TPU v7x, 32 devices: a whole 2x2x4 slice. The times are simulated.
32 devices in a mesh: section: 4 (over y, x), dp: 8 (over z, core).
Axes of the slice: x: 2, y: 2, z: 4, core: 2. Of those that a mesh axis runs over, the one named last changes fastest.
Arguments:
- buffer: bfloat16 [4, 64, 2048], P('section', 'dp'), may hold values from -6 to 6
- gate_weight: bfloat16 [4, 2, 2048, 8192], P('section', None, None, 'dp'), may hold values from -0.125 to 0.125
- up_weight: bfloat16 [4, 2, 2048, 8192], P('section', None, None, 'dp'), may hold values from -0.125 to 0.125
- down_weight: bfloat16 [4, 2, 8192, 2048], P('section', None, 'dp'), may hold values from -0.09375 to 0.09375
- norm_gain: float32 [4, 2, 2048], P('section'), may hold values from 0.1 to 1.9
- repeat_index: int32 [2, 4], P(None, 'section'), may hold values from 0 to 1
Outputs:
- final_buffer: bfloat16 [4, 64, 2048], P('section', 'dp')
Inputs may be any that keep to these rules, and one draw needn't show every extreme that they name: `repeat_index`: the layer each section applies, one of its 2.
All inputs are finite; a program needn't handle non-finite values.
Results may differ from a plain program's by a relative error of at most 0.01.
Values may be sent and summed in bfloat16 or wider, within the bound.
A program may use at most 128 MiB of HBM per device.

v0:
```python
import jax
import jax.numpy as jnp
from jax import lax
from jax.sharding import PartitionSpec as P

TICKS = 2


epsilon = 0.5


def from_partner(value, axis, bit):
    mask = 2**bit
    pairs = [(source, source ^ mask) for source in range(lax.axis_size(axis))]
    return lax.ppermute(value, axis, pairs)


def passed_along(block, axis, distance):
    devices = range(lax.axis_size(axis))
    route = [((i - distance) % len(devices), i) for i in devices]
    return lax.ppermute(block, axis, route)


def feed_forward(block_rows, gate_slab, up_slab, down_slab):
    gate_value = jnp.dot(block_rows, gate_slab, preferred_element_type=jnp.float32)
    up_value = jnp.dot(block_rows, up_slab, preferred_element_type=jnp.float32)
    hidden = (jax.nn.silu(gate_value) * up_value).astype(jnp.bfloat16)
    return jnp.dot(hidden, down_slab, preferred_element_type=jnp.float32)


def on_device(buffer, gate_weight, up_weight, down_weight, norm_gain, repeat_index):
    current = buffer[0]
    levels = lax.axis_size("dp").bit_length() - 1
    position = lax.axis_index("dp")
    for tick_index in range(TICKS):
        chosen = repeat_index[tick_index, 0]
        gate_slab = lax.dynamic_index_in_dim(gate_weight[0], chosen, 0, keepdims=False)
        up_slab = lax.dynamic_index_in_dim(up_weight[0], chosen, 0, keepdims=False)
        down_slab = lax.dynamic_index_in_dim(down_weight[0], chosen, 0, keepdims=False)
        gain_row = lax.dynamic_index_in_dim(norm_gain[0], chosen, 0, keepdims=False)
        widened = current.astype(jnp.float32)
        squares = jnp.mean(widened * widened, axis=-1, keepdims=True)
        normed = (widened * lax.rsqrt(squares + epsilon) * gain_row[None, :]).astype(jnp.bfloat16)
        paired = from_partner((gate_slab, up_slab, down_slab), "dp", 0)
        gate_both = jnp.concatenate([gate_slab, paired[0]], axis=1)
        up_both = jnp.concatenate([up_slab, paired[1]], axis=1)
        down_both = jnp.concatenate([down_slab, paired[2]], axis=0)
        group_block = normed
        for bit_number in range(1, levels):
            partner = from_partner(group_block, "dp", bit_number)
            upper_half = position >> bit_number & 1 == 1
            group_block = jnp.where(
                upper_half,
                jnp.concatenate([partner, group_block], axis=0),
                jnp.concatenate([group_block, partner], axis=0),
            )
        partial_value = feed_forward(group_block, gate_both, up_both, down_both)
        for bit_number in reversed(range(1, levels)):
            half_rows = partial_value.shape[0] // 2
            lower_part = partial_value[:half_rows]
            higher_part = partial_value[half_rows:]
            upper_half = position >> bit_number & 1 == 1
            kept_half = jnp.where(upper_half, higher_part, lower_part)
            sent_half = jnp.where(upper_half, lower_part, higher_part)
            partial_value = kept_half + from_partner(sent_half, "dp", bit_number)
        advanced = (widened + partial_value).astype(jnp.bfloat16)
        current = passed_along(advanced, "section", 1)
    return current[None]


def solution(mesh):
    placed = (
        P("section", "dp", None),
        P("section", None, None, "dp"),
        P("section", None, None, "dp"),
        P("section", None, "dp", None),
        P("section", None, None),
        P(None, "section"),
    )
    return jax.shard_map(
        on_device, mesh=mesh, in_specs=placed, out_specs=P("section", "dp", None), check_vma=False
    )
```

profile of v0, /device:TPU:0, one launch (start us, length us, event | category | flops | bytes accessed | tf_op | source)
XLA Modules:
  0.0 110.1 jit_solution(8566383915136789577)
XLA Ops:
  0.0 1.3 %fusion.50 = (s32[1,1]{0,1:T(1,128)}, s32[1,1]{0,1:T(1,128)}) fusion(s32[2,1]{0,1:T(1,128)} %param.11), kind=kLoop, calls=%fused_computation.68 | loop fusion | bytes 16 | tf_op jit(solution)/shard_map/slice | solution.py:36
  5.3 7.8 %dynamic-slice_bitcast_fusion.2 = (bf16[2048,1024]{1,0:T(8,128)(2,1)}, bf16[2048,1024]{1,0:T(8,128)(2,1)}) fusion(bf16[1,2,2048,1024]{3,2,1,0:T(8,128)(2,1)} %param.7, s32[]{:T(128)S(6)} %select_n.90, s32[]{:T(128)S(6)} %select_n.83), kind=kLoop, calls=%fused_computation.26 | loop fusion | bytes 16777224 | tf_op jit(solution)/shard_map/jit(dynamic_index_in_dim)/squeeze | solution.py:37
  13.7 4.2 %dynamic-slice_bitcast_fusion.1 = (bf16[2048,1024]{1,0:T(8,128)(2,1)}, bf16[2048,1024]{1,0:T(8,128)(2,1)}) fusion(bf16[1,2,2048,1024]{3,2,1,0:T(8,128)(2,1)S(1)} %copy-done, s32[]{:T(128)S(6)} %select_n.90, s32[]{:T(128)S(6)} %select_n.83), kind=kLoop, calls=%fused_computation.25 | loop fusion | bytes 16777224 | tf_op jit(solution)/shard_map/jit(dynamic_index_in_dim)/squeeze | solution.py:38
  17.9 8.5 %dynamic-slice_bitcast_fusion = (bf16[1024,2048]{1,0:T(8,128)(2,1)}, bf16[1024,2048]{1,0:T(8,128)(2,1)}) fusion(bf16[1,2,1024,2048]{3,2,1,0:T(8,128)(2,1)} %param.9, s32[]{:T(128)S(6)} %select_n.90, s32[]{:T(128)S(6)} %select_n.83), kind=kLoop, calls=%fused_computation.24 | loop fusion | bytes 16777224 | tf_op jit(solution)/shard_map/jit(dynamic_index_in_dim)/squeeze | solution.py:39
  27.1 2.6 %collective-permute-start = (bf16[8,2048]{1,0:T(8,128)(2,1)S(1)}, bf16[8,2048]{1,0:T(8,128)(2,1)S(1)}, u32[]{:S(2)}, u32[]{:S(2)}) collective-permute-start(bf16[8,2048]{1,0:T(8,128)(2,1)S(1)} %fusion.40), channel_id=1, source_target_pairs={{0,2},{1,3},{2,0},{3,1},{4,6},{5,7},{6,4},{7,5},{8,10},{9,11},{10,... | collective-permute-start | bytes 98312 | tf_op jit(solution)/shard_map/ppermute | solution.py:15
  29.7 2.0 %collective-permute-done = bf16[8,2048]{1,0:T(8,128)(2,1)S(1)} collective-permute-done((bf16[8,2048]{1,0:T(8,128)(2,1)S(1)}, bf16[8,2048]{1,0:T(8,128)(2,1)S(1)}, u32[]{:S(2)}, u32[]{:S(2)}) %collective-permute-start) | collective-permute-done | bytes 32800 | tf_op jit(solution)/shard_map/ppermute | solution.py:15
  31.8 2.9 %collective-permute-start.1 = (bf16[16,2048]{1,0:T(8,128)(2,1)S(1)}, bf16[16,2048]{1,0:T(8,128)(2,1)S(1)}, u32[]{:S(2)}, u32[]{:S(2)}) collective-permute-start(bf16[16,2048]{1,0:T(8,128)(2,1)S(1)} %maximum_select_fusion.2), channel_id=1, source_target_pairs={{0,4},{1,5},{2,6},{3,7},{4,0},{5,1},{6,2},{7,3},{8,12},{9,13},{10,... | collective-permute-start | bytes 196616 | tf_op jit(solution)/shard_map/ppermute | solution.py:15
  34.7 2.7 %collective-permute-done.1 = bf16[16,2048]{1,0:T(8,128)(2,1)S(1)} collective-permute-done((bf16[16,2048]{1,0:T(8,128)(2,1)S(1)}, bf16[16,2048]{1,0:T(8,128)(2,1)S(1)}, u32[]{:S(2)}, u32[]{:S(2)}) %collective-permute-start.1) | collective-permute-done | bytes 65568 | tf_op jit(solution)/shard_map/ppermute | solution.py:15
  37.9 4.3 %fusion = f32[32,2048]{1,0:T(8,128)S(1)} fusion(bf16[2048,1024]{1,0:T(8,128)(2,1)} %collective-permute-done.2, bf16[2048,1024]{1,0:T(8,128)(2,1)} %get-tuple-element.8, bf16[16,2048]{1,0:T(8,128)(2,1)S(1)} %maximum_select_fusion.2, bf16[16,2048]{1,0:T(8,128)(2,1)S(1)} %collective-permute-done.1, pred[]{:T(512)S(6)} %eq.5), kind=kOutput, calls=%fused_computation | convolution fusion | flops 285802496 | bytes 8781825 | tf_op jit(solution)/shard_map/dot_general | solution.py:25
  42.2 8.9 %fusion.8 = f32[32,2048]{1,0:T(8,128)S(1)} fusion(bf16[1024,2048]{1,0:T(8,128)(2,1)} %collective-permute-done.4, bf16[1024,2048]{1,0:T(8,128)(2,1)} %get-tuple-element.10, f32[32,2048]{1,0:T(8,128)S(1)} %fusion, bf16[2048,1024]{1,0:T(8,128)(2,1)} %collective-permute-done.3, bf16[2048,1024]{1,0:T(8,128)(2,1)} %get-tuple-element.6, ...), kind=kOutput, calls=%fused_computation.8 | convolution fusion | flops 571408384 | bytes 17432576 | tf_op jit(solution)/shard_map/dot_general | solution.py:28
  51.1 2.6 %collective-permute-start.5 = (f32[16,2048]{1,0:T(8,128)S(1)}, f32[16,2048]{1,0:T(8,128)S(1)}, u32[]{:S(2)}, u32[]{:S(2)}) collective-permute-start(f32[16,2048]{1,0:T(8,128)S(1)} %slice_select_fusion.1), channel_id=1, source_target_pairs={{0,4},{1,5},{2,6},{3,7},{4,0},{5,1},{6,2},{7,3},{8,12},{9,13},{10,... | collective-permute-start | bytes 393224 | tf_op jit(solution)/shard_map/ppermute | solution.py:15
  53.8 6.5 %collective-permute-done.5 = f32[16,2048]{1,0:T(8,128)S(1)} collective-permute-done((f32[16,2048]{1,0:T(8,128)S(1)}, f32[16,2048]{1,0:T(8,128)S(1)}, u32[]{:S(2)}, u32[]{:S(2)}) %collective-permute-start.5) | collective-permute-done | bytes 131104 | tf_op jit(solution)/shard_map/ppermute | solution.py:15
  61.1 3.6 %collective-permute-done.6 = f32[8,2048]{1,0:T(8,128)S(1)} collective-permute-done((f32[8,2048]{1,0:T(8,128)S(1)}, f32[8,2048]{1,0:T(8,128)S(1)}, u32[]{:S(2)}, u32[]{:S(2)}) %collective-permute-start.6) | collective-permute-done | bytes 65568 | tf_op jit(solution)/shard_map/ppermute | solution.py:15
  64.7 1.5 %collective-permute-start.7 = (bf16[8,2048]{1,0:T(8,128)(2,1)S(1)}, bf16[8,2048]{1,0:T(8,128)(2,1)S(1)}, u32[]{:S(2)}, u32[]{:S(2)}) collective-permute-start(bf16[8,2048]{1,0:T(8,128)(2,1)S(1)} %fusion.41), channel_id=1, source_target_pairs={{24,0},{0,8},{8,16},{16,24},{25,1},{1,9},{9,17},{17,25},{26,2},{2,... | collective-permute-start | bytes 98312 | tf_op jit(solution)/shard_map/ppermute | solution.py:21
  66.3 3.3 %collective-permute-done.7 = bf16[8,2048]{1,0:T(8,128)(2,1)S(1)} collective-permute-done((bf16[8,2048]{1,0:T(8,128)(2,1)S(1)}, bf16[8,2048]{1,0:T(8,128)(2,1)S(1)}, u32[]{:S(2)}, u32[]{:S(2)}) %collective-permute-start.7) | collective-permute-done | bytes 32800 | tf_op jit(solution)/shard_map/ppermute | solution.py:21
  70.5 3.3 %collective-permute-done.8 = bf16[8,2048]{1,0:T(8,128)(2,1)S(1)} collective-permute-done((bf16[8,2048]{1,0:T(8,128)(2,1)S(1)}, bf16[8,2048]{1,0:T(8,128)(2,1)S(1)}, u32[]{:S(2)}, u32[]{:S(2)}) %collective-permute-start.8) | collective-permute-done | bytes 32800 | tf_op jit(solution)/shard_map/ppermute | solution.py:15
  73.8 2.5 %collective-permute-start.9 = (bf16[16,2048]{1,0:T(8,128)(2,1)S(1)}, bf16[16,2048]{1,0:T(8,128)(2,1)S(1)}, u32[]{:S(2)}, u32[]{:S(2)}) collective-permute-start(bf16[16,2048]{1,0:T(8,128)(2,1)S(1)} %maximum_select_fusion.3), channel_id=1, source_target_pairs={{0,4},{1,5},{2,6},{3,7},{4,0},{5,1},{6,2},{7,3},{8,12},{9,13},{10,... | collective-permute-start | bytes 196616 | tf_op jit(solution)/shard_map/ppermute | solution.py:15
  76.2 3.5 %collective-permute-done.9 = bf16[16,2048]{1,0:T(8,128)(2,1)S(1)} collective-permute-done((bf16[16,2048]{1,0:T(8,128)(2,1)S(1)}, bf16[16,2048]{1,0:T(8,128)(2,1)S(1)}, u32[]{:S(2)}, u32[]{:S(2)}) %collective-permute-start.9) | collective-permute-done | bytes 65568 | tf_op jit(solution)/shard_map/ppermute | solution.py:15
  79.7 4.3 %fusion.12 = f32[32,2048]{1,0:T(8,128)S(1)} fusion(bf16[2048,1024]{1,0:T(8,128)(2,1)} %collective-permute-done.10, bf16[2048,1024]{1,0:T(8,128)(2,1)} %get-tuple-element.7, bf16[16,2048]{1,0:T(8,128)(2,1)S(1)} %maximum_select_fusion.3, bf16[16,2048]{1,0:T(8,128)(2,1)S(1)} %collective-permute-done.9, pred[]{:T(512)S(6)} %eq.5), kind=kOutput, calls=%fused_computation.12 | convolution fusion | flops 285802496 | bytes 8781825 | tf_op jit(solution)/shard_map/dot_general | solution.py:25
  84.0 8.9 %fusion.20 = f32[32,2048]{1,0:T(8,128)S(1)} fusion(bf16[1024,2048]{1,0:T(8,128)(2,1)} %collective-permute-done.12, bf16[1024,2048]{1,0:T(8,128)(2,1)} %get-tuple-element.9, f32[32,2048]{1,0:T(8,128)S(1)} %fusion.12, bf16[2048,1024]{1,0:T(8,128)(2,1)} %collective-permute-done.11, bf16[2048,1024]{1,0:T(8,128)(2,1)} %get-tuple-element.5, ...), kind=kOutput, calls=%fused_computation.20 | convolution fusion | flops 571408384 | bytes 17432576 | tf_op jit(solution)/shard_map/dot_general | solution.py:28
  92.9 1.8 %collective-permute-start.13 = (f32[16,2048]{1,0:T(8,128)S(1)}, f32[16,2048]{1,0:T(8,128)S(1)}, u32[]{:S(2)}, u32[]{:S(2)}) collective-permute-start(f32[16,2048]{1,0:T(8,128)S(1)} %slice_select_fusion), channel_id=1, source_target_pairs={{0,4},{1,5},{2,6},{3,7},{4,0},{5,1},{6,2},{7,3},{8,12},{9,13},{10,... | collective-permute-start | bytes 393224 | tf_op jit(solution)/shard_map/ppermute | solution.py:15
  94.7 5.5 %collective-permute-done.13 = f32[16,2048]{1,0:T(8,128)S(1)} collective-permute-done((f32[16,2048]{1,0:T(8,128)S(1)}, f32[16,2048]{1,0:T(8,128)S(1)}, u32[]{:S(2)}, u32[]{:S(2)}) %collective-permute-start.13) | collective-permute-done | bytes 131104 | tf_op jit(solution)/shard_map/ppermute | solution.py:15
  100.6 4.0 %collective-permute-done.14 = f32[8,2048]{1,0:T(8,128)S(1)} collective-permute-done((f32[8,2048]{1,0:T(8,128)S(1)}, f32[8,2048]{1,0:T(8,128)S(1)}, u32[]{:S(2)}, u32[]{:S(2)}) %collective-permute-start.14) | collective-permute-done | bytes 65568 | tf_op jit(solution)/shard_map/ppermute | solution.py:15
  105.3 4.2 %collective-permute-done.15 = bf16[8,2048]{1,0:T(8,128)(2,1)S(1)} collective-permute-done((bf16[8,2048]{1,0:T(8,128)(2,1)S(1)}, bf16[8,2048]{1,0:T(8,128)(2,1)S(1)}, u32[]{:S(2)}, u32[]{:S(2)}) %collective-permute-start.15) | collective-permute-done | bytes 32800 | tf_op jit(solution)/shard_map/ppermute | solution.py:21
  (40 shorter events, 5.1 us)
Async XLA Ops:
  5.3 8.3 %copy-start = (bf16[1,2,2048,1024]{3,2,1,0:T(8,128)(2,1)S(1)}, bf16[1,2,2048,1024]{3,2,1,0:T(8,128)(2,1)}, u32[]{:S(2)}) copy-start(bf16[1,2,2048,1024]{3,2,1,0:T(8,128)(2,1)} %param.8) | copy-start | bytes 25165828
  13.2 24.2 %collective-permute-start.2 = (bf16[2048,1024]{1,0:T(8,128)(2,1)}, bf16[2048,1024]{1,0:T(8,128)(2,1)}, u32[]{:S(2)}, u32[]{:S(2)}) collective-permute-start(bf16[2048,1024]{1,0:T(8,128)(2,1)} %get-tuple-element.8), channel_id=1, source_target_pairs={{0,1},{1,0},{2,3},{3,2},{4,5},{5,4},{6,7},{7,6},{8,9},{9,8},{10,11... | collective-permute-start | bytes 12582920 | tf_op jit(solution)/shard_map/ppermute | solution.py:15
  17.9 9.0 %copy-start.1 = (bf16[1,8,2048]{2,1,0:T(8,128)(2,1)S(1)}, bf16[1,8,2048]{2,1,0:T(8,128)(2,1)}, u32[]{:S(2)}) copy-start(bf16[1,8,2048]{2,1,0:T(8,128)(2,1)} %param.6) | copy-start | bytes 98308
  17.9 9.1 %copy-start.2 = (f32[1,2,2048]{2,1,0:T(2,128)S(1)}, f32[1,2,2048]{2,1,0:T(2,128)}, u32[]{:S(2)}) copy-start(f32[1,2,2048]{2,1,0:T(2,128)} %param.10) | copy-start | bytes 49156
  17.9 24.3 %collective-permute-start.3 = (bf16[2048,1024]{1,0:T(8,128)(2,1)}, bf16[2048,1024]{1,0:T(8,128)(2,1)}, u32[]{:S(2)}, u32[]{:S(2)}) collective-permute-start(bf16[2048,1024]{1,0:T(8,128)(2,1)} %get-tuple-element.6), channel_id=1, source_target_pairs={{0,1},{1,0},{2,3},{3,2},{4,5},{5,4},{6,7},{7,6},{8,9},{9,8},{10,11... | collective-permute-start | bytes 12582920 | tf_op jit(solution)/shard_map/ppermute | solution.py:15
  26.4 15.9 %collective-permute-start.4 = (bf16[1024,2048]{1,0:T(8,128)(2,1)}, bf16[1024,2048]{1,0:T(8,128)(2,1)}, u32[]{:S(2)}, u32[]{:S(2)}) collective-permute-start(bf16[1024,2048]{1,0:T(8,128)(2,1)} %get-tuple-element.10), channel_id=1, source_target_pairs={{0,1},{1,0},{2,3},{3,2},{4,5},{5,4},{6,7},{7,6},{8,9},{9,8},{10,11... | collective-permute-start | bytes 12582920 | tf_op jit(solution)/shard_map/ppermute | solution.py:15
  27.1 4.7 %collective-permute-start = (bf16[8,2048]{1,0:T(8,128)(2,1)S(1)}, bf16[8,2048]{1,0:T(8,128)(2,1)S(1)}, u32[]{:S(2)}, u32[]{:S(2)}) collective-permute-start(bf16[8,2048]{1,0:T(8,128)(2,1)S(1)} %fusion.40), channel_id=1, source_target_pairs={{0,2},{1,3},{2,0},{3,1},{4,6},{5,7},{6,4},{7,5},{8,10},{9,11},{10,... | collective-permute-start | bytes 98312 | tf_op jit(solution)/shard_map/ppermute | solution.py:15
  31.8 5.6 %collective-permute-start.1 = (bf16[16,2048]{1,0:T(8,128)(2,1)S(1)}, bf16[16,2048]{1,0:T(8,128)(2,1)S(1)}, u32[]{:S(2)}, u32[]{:S(2)}) collective-permute-start(bf16[16,2048]{1,0:T(8,128)(2,1)S(1)} %maximum_select_fusion.2), channel_id=1, source_target_pairs={{0,4},{1,5},{2,6},{3,7},{4,0},{5,1},{6,2},{7,3},{8,12},{9,13},{10,... | collective-permute-start | bytes 196616 | tf_op jit(solution)/shard_map/ppermute | solution.py:15
  34.7 41.5 %collective-permute-start.10 = (bf16[2048,1024]{1,0:T(8,128)(2,1)}, bf16[2048,1024]{1,0:T(8,128)(2,1)}, u32[]{:S(2)}, u32[]{:S(2)}) collective-permute-start(bf16[2048,1024]{1,0:T(8,128)(2,1)} %get-tuple-element.7), channel_id=1, source_target_pairs={{0,1},{1,0},{2,3},{3,2},{4,5},{5,4},{6,7},{7,6},{8,9},{9,8},{10,11... | collective-permute-start | bytes 12582920 | tf_op jit(solution)/shard_map/ppermute | solution.py:15
  37.4 46.6 %collective-permute-start.11 = (bf16[2048,1024]{1,0:T(8,128)(2,1)}, bf16[2048,1024]{1,0:T(8,128)(2,1)}, u32[]{:S(2)}, u32[]{:S(2)}) collective-permute-start(bf16[2048,1024]{1,0:T(8,128)(2,1)} %get-tuple-element.5), channel_id=1, source_target_pairs={{0,1},{1,0},{2,3},{3,2},{4,5},{5,4},{6,7},{7,6},{8,9},{9,8},{10,11... | collective-permute-start | bytes 12582920 | tf_op jit(solution)/shard_map/ppermute | solution.py:15
  37.4 46.6 %collective-permute-start.12 = (bf16[1024,2048]{1,0:T(8,128)(2,1)}, bf16[1024,2048]{1,0:T(8,128)(2,1)}, u32[]{:S(2)}, u32[]{:S(2)}) collective-permute-start(bf16[1024,2048]{1,0:T(8,128)(2,1)} %get-tuple-element.9), channel_id=1, source_target_pairs={{0,1},{1,0},{2,3},{3,2},{4,5},{5,4},{6,7},{7,6},{8,9},{9,8},{10,11... | collective-permute-start | bytes 12582920 | tf_op jit(solution)/shard_map/ppermute | solution.py:15
  51.1 9.2 %collective-permute-start.5 = (f32[16,2048]{1,0:T(8,128)S(1)}, f32[16,2048]{1,0:T(8,128)S(1)}, u32[]{:S(2)}, u32[]{:S(2)}) collective-permute-start(f32[16,2048]{1,0:T(8,128)S(1)} %slice_select_fusion.1), channel_id=1, source_target_pairs={{0,4},{1,5},{2,6},{3,7},{4,0},{5,1},{6,2},{7,3},{8,12},{9,13},{10,... | collective-permute-start | bytes 393224 | tf_op jit(solution)/shard_map/ppermute | solution.py:15
  60.4 4.3 %collective-permute-start.6 = (f32[8,2048]{1,0:T(8,128)S(1)}, f32[8,2048]{1,0:T(8,128)S(1)}, u32[]{:S(2)}, u32[]{:S(2)}) collective-permute-start(f32[8,2048]{1,0:T(8,128)S(1)} %slice_select_fusion.3), channel_id=1, source_target_pairs={{0,2},{1,3},{2,0},{3,1},{4,6},{5,7},{6,4},{7,5},{8,10},{9,11},{10,... | collective-permute-start | bytes 196616 | tf_op jit(solution)/shard_map/ppermute | solution.py:15
  64.7 4.9 %collective-permute-start.7 = (bf16[8,2048]{1,0:T(8,128)(2,1)S(1)}, bf16[8,2048]{1,0:T(8,128)(2,1)S(1)}, u32[]{:S(2)}, u32[]{:S(2)}) collective-permute-start(bf16[8,2048]{1,0:T(8,128)(2,1)S(1)} %fusion.41), channel_id=1, source_target_pairs={{24,0},{0,8},{8,16},{16,24},{25,1},{1,9},{9,17},{17,25},{26,2},{2,... | collective-permute-start | bytes 98312 | tf_op jit(solution)/shard_map/ppermute | solution.py:21
  69.8 4.0 %collective-permute-start.8 = (bf16[8,2048]{1,0:T(8,128)(2,1)S(1)}, bf16[8,2048]{1,0:T(8,128)(2,1)S(1)}, u32[]{:S(2)}, u32[]{:S(2)}) collective-permute-start(bf16[8,2048]{1,0:T(8,128)(2,1)S(1)} %fusion.36), channel_id=1, source_target_pairs={{0,2},{1,3},{2,0},{3,1},{4,6},{5,7},{6,4},{7,5},{8,10},{9,11},{10,... | collective-permute-start | bytes 98312 | tf_op jit(solution)/shard_map/ppermute | solution.py:15
  73.8 5.9 %collective-permute-start.9 = (bf16[16,2048]{1,0:T(8,128)(2,1)S(1)}, bf16[16,2048]{1,0:T(8,128)(2,1)S(1)}, u32[]{:S(2)}, u32[]{:S(2)}) collective-permute-start(bf16[16,2048]{1,0:T(8,128)(2,1)S(1)} %maximum_select_fusion.3), channel_id=1, source_target_pairs={{0,4},{1,5},{2,6},{3,7},{4,0},{5,1},{6,2},{7,3},{8,12},{9,13},{10,... | collective-permute-start | bytes 196616 | tf_op jit(solution)/shard_map/ppermute | solution.py:15
  92.9 7.3 %collective-permute-start.13 = (f32[16,2048]{1,0:T(8,128)S(1)}, f32[16,2048]{1,0:T(8,128)S(1)}, u32[]{:S(2)}, u32[]{:S(2)}) collective-permute-start(f32[16,2048]{1,0:T(8,128)S(1)} %slice_select_fusion), channel_id=1, source_target_pairs={{0,4},{1,5},{2,6},{3,7},{4,0},{5,1},{6,2},{7,3},{8,12},{9,13},{10,... | collective-permute-start | bytes 393224 | tf_op jit(solution)/shard_map/ppermute | solution.py:15
  100.3 4.3 %collective-permute-start.14 = (f32[8,2048]{1,0:T(8,128)S(1)}, f32[8,2048]{1,0:T(8,128)S(1)}, u32[]{:S(2)}, u32[]{:S(2)}) collective-permute-start(f32[8,2048]{1,0:T(8,128)S(1)} %slice_select_fusion.2), channel_id=1, source_target_pairs={{0,2},{1,3},{2,0},{3,1},{4,6},{5,7},{6,4},{7,5},{8,10},{9,11},{10,... | collective-permute-start | bytes 196616 | tf_op jit(solution)/shard_map/ppermute | solution.py:15
  104.6 4.9 %collective-permute-start.15 = (bf16[8,2048]{1,0:T(8,128)(2,1)S(1)}, bf16[8,2048]{1,0:T(8,128)(2,1)S(1)}, u32[]{:S(2)}, u32[]{:S(2)}) collective-permute-start(bf16[8,2048]{1,0:T(8,128)(2,1)S(1)} %fusion.37), channel_id=1, source_target_pairs={{24,0},{0,8},{8,16},{16,24},{25,1},{1,9},{9,17},{17,25},{26,2},{2,... | collective-permute-start | bytes 98312 | tf_op jit(solution)/shard_map/ppermute | solution.py:21
where the time goes:
time: 110 us
  waiting for transfers between devices  38.7 us (35%)
  matrix products  26.3 us (24%)
  local copies, waits for them, and re-layouts  22.5 us (20%)
  starting transfers between devices  17.9 us (16%)
  between operations  4.13 us (4%)
    ppermute x14, waiting for transfers between devices, from_partner(): return lax.ppermute(value, axis, pairs)  31.2 us
    dot_general x2, matrix products, feed_forward(): return jnp.dot(hidden, down_slab, preferred_element_type=jnp.float32)  17.7 us
    ppermute x14, starting transfers between devices, from_partner(): return lax.ppermute(value, axis, pairs)  15.7 us
    dot_general x2, matrix products, feed_forward(): jnp.dot(block_rows, gate_slab, preferred_element_type=jnp.float32)  8.59 us
    squeeze x1, local copies, waits for them, and re-layouts, on_device(): lax.dynamic_index_in_dim(down_weight[0], chosen, 0, keepdims=False)  8.47 us
    squeeze x1, local copies, waits for them, and re-layouts, on_device(): lax.dynamic_index_in_dim(gate_weight[0], chosen, 0, keepdims=False)  7.84 us
    ppermute x2, waiting for transfers between devices, passed_along(): return lax.ppermute(block, axis, route)  7.53 us
    squeeze x1, local copies, waits for them, and re-layouts, on_device(): up_slab = lax.dynamic_index_in_dim(up_weight[0], chosen, 0, keepdims=False)  4.19 us
  transfers between devices with their start and end apart: 16, of which 10 were waited for; matrix products, arithmetic and copies ran while one was open for 28% of the time, Pallas kernels for 0%

commit v1 on v0

v1 whole, which is shorter than its diff:
```python
import functools

import jax
import jax.numpy as jnp
from jax import lax
from jax.experimental import pallas as pl
from jax.experimental.pallas import tpu as pltpu
from jax.sharding import PartitionSpec as P

MESH = pl.DeviceIdType.MESH
EPSILON = 0.5
GATE_COLUMNS = 256
DOWN_CHUNKS = 4


def flipped(value, mask):
    bit = 1
    while bit <= mask:
        if mask & bit:
            value = value + bit - 2 * bit * (lax.div(value, bit) % 2)
        bit *= 2
    return value


def relay(dims, index_ref, buffer_ref, gain_ref, gate_hbm, up_hbm, down_hbm, out_ref, *scratch):
    ns, nd, ticks, rows, width, gate_chunks, gate_cols, down_chunks, down_cols = dims
    nz = nd // 2
    scratch = list(scratch)
    gates = [scratch.pop(0) for _ in range(gate_chunks)]
    ups = [scratch.pop(0) for _ in range(gate_chunks)]
    downs = [scratch.pop(0) for _ in range(down_chunks)]
    (blocks, normed, hidden, partial, paired, summed, landed, advanced,
     gate_sem, up_sem, down_sem, spread_send, forward_send, block_recv,
     pair_send, pair_recv, row_send, row_recv, shift_send, shift_recv) = scratch

    s = lax.axis_index("section")
    d = lax.axis_index("dp")
    z = lax.div(d, 2)
    core = lax.rem(d, 2)
    other = z * 2 + 1 - core
    after = lax.rem(s + 1, ns)
    before = lax.rem(s + ns - 1, ns)

    def dev(section, position):
        return {"section": section, "dp": position}

    def at(zz):
        return zz * 2 + core

    loads = []
    for i in range(gate_chunks):
        cols = pl.ds(i * gate_cols, gate_cols)
        loads.append(pltpu.make_async_copy(gate_hbm.at[0, :, :, cols], gates[i], gate_sem.at[i]))
        loads.append(pltpu.make_async_copy(up_hbm.at[0, :, :, cols], ups[i], up_sem.at[i]))
    for c in range(down_chunks):
        cols = pl.ds(c * down_cols, down_cols)
        loads.append(pltpu.make_async_copy(down_hbm.at[0, :, :, cols], downs[c], down_sem.at[c]))
    for load in loads:
        load.start()

    barrier = pltpu.get_barrier_semaphore()
    pl.semaphore_signal(barrier, inc=1, device_id=dev(s, other), device_id_type=MESH)
    for j in range(1, nz):
        pl.semaphore_signal(barrier, inc=1, device_id=dev(s, at(flipped(z, j))), device_id_type=MESH)
    for j in range(nz):
        zz = flipped(z, j)
        pl.semaphore_signal(barrier, inc=1, device_id=dev(after, at(zz)), device_id_type=MESH)
        pl.semaphore_signal(barrier, inc=1, device_id=dev(before, at(zz)), device_id_type=MESH)
    pl.semaphore_wait(barrier, 3 * nz)

    sent = []

    def send(src, dst, send_sem, recv_sem, device):
        copy = pltpu.make_async_remote_copy(
            src_ref=src, dst_ref=dst, send_sem=send_sem, recv_sem=recv_sem,
            device_id=device, device_id_type=MESH,
        )
        copy.start()
        sent.append(copy)

    def arrived(dst, recv_sem):
        pltpu.make_async_remote_copy(
            src_ref=dst, dst_ref=dst, send_sem=shift_send, recv_sem=recv_sem,
            device_id=dev(s, other), device_id_type=MESH,
        ).wait_recv()

    for t in range(ticks):
        layer = index_ref[t, 0]
        if t == 0:
            for j in reversed(range(1, nz)):
                send(buffer_ref.at[0], blocks.at[t, d], spread_send.at[t, j], block_recv.at[t, d],
                     dev(s, at(flipped(z, j))))
            send(buffer_ref.at[0], blocks.at[t, d], forward_send.at[t, 0], block_recv.at[t, d], dev(s, other))
            blocks[t, d] = buffer_ref[0]
        else:
            for j in reversed(range(nz)):
                send(advanced.at[t - 1], blocks.at[t, d], spread_send.at[t, j], block_recv.at[t, d],
                     dev(after, at(flipped(z, j))))
        for j in range(nz):
            slot = at(flipped(z, j))
            if t > 0 or j > 0:
                arrived(blocks.at[t, slot], block_recv.at[t, slot])
                send(blocks.at[t, slot], blocks.at[t, slot], forward_send.at[t, j], block_recv.at[t, slot],
                     dev(s, other))
        gain = gain_ref[0, pl.ds(layer, 1), :]
        for j in range(nz):
            zz = flipped(z, j)
            slot = zz * 2 + 1 - core
            arrived(blocks.at[t, slot], block_recv.at[t, slot])
            value = jnp.concatenate(
                [blocks[t, zz * 2].astype(jnp.float32), blocks[t, zz * 2 + 1].astype(jnp.float32)], axis=0
            )
            squares = jnp.mean(value * value, axis=-1, keepdims=True)
            normed[zz] = (value * lax.rsqrt(squares + EPSILON) * gain).astype(jnp.bfloat16)

        for i in range(gate_chunks):
            if t == 0:
                loads[2 * i].wait()
                loads[2 * i + 1].wait()
            tokens = normed[...].reshape(nd * rows, width)
            gate = jnp.dot(tokens, gates[i][layer], preferred_element_type=jnp.float32)
            up = jnp.dot(tokens, ups[i][layer], preferred_element_type=jnp.float32)
            hidden[:, i * gate_cols:(i + 1) * gate_cols] = (
                gate / (1.0 + jnp.exp(-gate)) * up
            ).astype(jnp.bfloat16)

        def scatter(c):
            arrived(paired.at[t, c], pair_recv.at[t, c])
            summed[t, c] = (partial[t, c, core] + paired[t, c]).astype(jnp.bfloat16)
            for j in reversed(range(1, nz)):
                zz = flipped(z, j)
                send(summed.at[t, c, zz], landed.at[t, c, z], row_send.at[t, c, j], row_recv.at[t, c, z],
                     dev(s, at(zz)))

        for c in range(down_chunks):
            if t == 0:
                loads[2 * gate_chunks + c].wait()
            part = jnp.dot(hidden[...], downs[c][layer], preferred_element_type=jnp.float32)
            part = part.reshape(nz, 2, rows, down_cols)
            partial[t, c, 0] = part[:, 0]
            partial[t, c, 1] = part[:, 1]
            send(partial.at[t, c, 1 - core], paired.at[t, c], pair_send.at[t, c], pair_recv.at[t, c],
                 dev(s, other))
            if c > 0:
                scatter(c - 1)
        scatter(down_chunks - 1)

        for c in range(down_chunks):
            total = partial[t, c, core, z] + paired[t, c, z]
            for j in range(1, nz):
                zz = flipped(z, j)
                arrived(landed.at[t, c, zz], row_recv.at[t, c, zz])
                total = total + landed[t, c, zz].astype(jnp.float32)
            cols = slice(c * down_cols, (c + 1) * down_cols)
            advanced[t, :, cols] = (blocks[t, d, :, cols].astype(jnp.float32) + total).astype(jnp.bfloat16)

    send(advanced.at[ticks - 1], out_ref.at[0], shift_send, shift_recv, dev(after, d))
    arrived(out_ref.at[0], shift_recv)
    for copy in sent:
        copy.wait_send()


def on_device(buffer, gate_weight, up_weight, down_weight, norm_gain, repeat_index):
    ns, nd = lax.axis_size("section"), lax.axis_size("dp")
    ticks = repeat_index.shape[0]
    _, rows, width = buffer.shape
    layers, units = gate_weight.shape[1], gate_weight.shape[3]
    nz = nd // 2
    gate_cols = min(GATE_COLUMNS, units)
    gate_chunks = units // gate_cols
    down_chunks = DOWN_CHUNKS
    down_cols = width // down_chunks
    dims = (ns, nd, ticks, rows, width, gate_chunks, gate_cols, down_chunks, down_cols)
    bf16, f32, DMA = jnp.bfloat16, jnp.float32, pltpu.SemaphoreType.DMA
    scratch = (
        [pltpu.VMEM((layers, width, gate_cols), bf16)] * (2 * gate_chunks)
        + [pltpu.VMEM((layers, units, down_cols), bf16)] * down_chunks
        + [
            pltpu.VMEM((ticks, nd, rows, width), bf16),
            pltpu.VMEM((nz, 2 * rows, width), bf16),
            pltpu.VMEM((nd * rows, units), bf16),
            pltpu.VMEM((ticks, down_chunks, 2, nz, rows, down_cols), f32),
            pltpu.VMEM((ticks, down_chunks, nz, rows, down_cols), f32),
            pltpu.VMEM((ticks, down_chunks, nz, rows, down_cols), bf16),
            pltpu.VMEM((ticks, down_chunks, nz, rows, down_cols), bf16),
            pltpu.VMEM((ticks, rows, width), bf16),
            DMA((gate_chunks,)), DMA((gate_chunks,)), DMA((down_chunks,)),
            DMA((ticks, nz)), DMA((ticks, nz)), DMA((ticks, nd)),
            DMA((ticks, down_chunks)), DMA((ticks, down_chunks)),
            DMA((ticks, down_chunks, nz)), DMA((ticks, down_chunks, nz)),
            DMA, DMA,
        ]
    )
    vmem = pl.BlockSpec(memory_space=pltpu.VMEM)
    smem = pl.BlockSpec(memory_space=pltpu.SMEM)
    hbm = pl.BlockSpec(memory_space=pl.ANY)
    return pl.pallas_call(
        functools.partial(relay, dims),
        out_shape=jax.ShapeDtypeStruct(buffer.shape, buffer.dtype),
        in_specs=[smem, vmem, vmem, hbm, hbm, hbm],
        out_specs=vmem,
        scratch_shapes=scratch,
        compiler_params=pltpu.CompilerParams(
            collective_id=0, has_side_effects=True, vmem_limit_bytes=60_000_000
        ),
    )(repeat_index, buffer, norm_gain, gate_weight, up_weight, down_weight)


def solution(mesh):
    placed = (
        P("section", "dp", None),
        P("section", None, None, "dp"),
        P("section", None, None, "dp"),
        P("section", None, "dp", None),
        P("section", None, None),
        P(None, "section"),
    )
    return jax.shard_map(
        on_device, mesh=mesh, in_specs=placed, out_specs=P("section", "dp", None), check_vma=False
    )
```

time: 110 us -> 42.9 us (0.39)
  Pallas kernels: 0 us -> 40 us
  waiting for transfers between devices: 38.7 us -> 0 us
  matrix products: 26.3 us -> 0 us
  local copies, waits for them, and re-layouts: 22.5 us -> 2.67 us
  starting transfers between devices: 17.9 us -> 0 us
  between operations: 4.13 us -> 0.01 us
    pallas_call x0 -> x1, Pallas kernels: none -> 40 us  [on_device(): pl.pallas_call(functools.partial(relay, dims), out_shape=jax.ShapeDtypeSt...]
    ppermute x16 -> x0, waiting for transfers between devices: 38.7 us -> none  [the longest x14 31.2 us: from_partner(): return lax.ppermute(value, axis, pairs)]
    dot_general x4 -> x0, matrix products: 26.3 us -> none  [the longest x2 17.7 us: feed_forward(): return jnp.dot(hidden, down_slab, preferred_element_type=jnp.float32)]
    squeeze x3 -> x0, local copies, waits for them, and re-layouts: 20.5 us -> none  [the longest x1 8.47 us: on_device(): lax.dynamic_index_in_dim(down_weight[0], chosen, 0, keepdims=False)]
    ppermute x16 -> x0, starting transfers between devices: 17.9 us -> none  [the longest x14 15.7 us: from_partner(): return lax.ppermute(value, axis, pairs)]
    unnamed x7 -> x2, local copies, waits for them, and re-layouts: 0.63 us -> 2.67 us
    slice x1 -> x0, local copies, waits for them, and re-layouts: 1.32 us -> none  [on_device(): chosen = repeat_index[tick_index, 0]]
  transfers between devices with their start and end apart: 16 -> 0, of which waited for: 10 -> 0; matrix products, arithmetic and copies ran while one was open for 28% -> 0% of each run, Pallas kernels for 0% -> 0%
where the time goes in v1:
time: 42.9 us; the launch traced here: 42.6 us
  Pallas kernels  40 us (93%)
  local copies, waits for them, and re-layouts  2.67 us (6%)
    pallas_call x1, Pallas kernels, on_device(): pl.pallas_call(functools.partial(relay, dims), out_shape=jax.ShapeDtypeSt...  40 us
    unnamed x2, local copies, waits for them, and re-layouts  2.67 us

profile of v1, /device:TPU:0, one launch (start us, length us, event | category | flops | bytes accessed | tf_op | source)
XLA Modules:
  0.0 42.6 jit_solution(7518963100725721302)
XLA Ops:
  0.0 1.3 %copy.7.index_ref = s32[2,1]{1,0:T(2,128)} copy(s32[2,1]{0,1:T(1,128)} %param.11) | data formatting | bytes 16 | tf_op args[5]
  1.3 40.0 %shard_map.64 = bf16[1,8,2048]{2,1,0:T(8,128)(2,1)} custom-call(s32[2,1]{1,0:T(2,128)} %copy.7.index_ref, bf16[1,8,2048]{2,1,0:T(8,128)(2,1)} %buffer_ref.1, f32[1,2,2048]{2,1,0:T(2,128)} %gain_ref.1, bf16[1,2,2048,1024]{3,2,1,0:T(8,128)(2,1)} %gate_hbm.1, bf16[1,2,2048,1024]{3,2,1,0:T(8,128)(2,1)} %up_hbm.1, bf16[1,2,1024,2048]{3,2,1,0:T(8,128)(2,1)} %down_hbm.1), custom_call_target="tpu_custom_call" | custom-call | tf_op jit(solution)/shard_map/pallas_call | solution.py:197
  41.3 1.4 %copy.9 = bf16[1,8,2048]{2,1,0:T(8,128)(2,1)} copy(bf16[1,8,2048]{2,1,0:T(8,128)(2,1)} %shard_map.64) | data formatting | bytes 65536

commit v2 on v1

--- a/solution.py
+++ b/solution.py
@@ -9,8 +9,8 @@
 
 MESH = pl.DeviceIdType.MESH
 EPSILON = 0.5
-GATE_COLUMNS = 256
-DOWN_CHUNKS = 4
+GATE_COLUMNS = 512
+DOWN_CHUNKS = 2
 
 
 def flipped(value, mask):
@@ -22,7 +22,7 @@
     return value
 
 
-def relay(dims, index_ref, buffer_ref, gain_ref, gate_hbm, up_hbm, down_hbm, out_ref, *scratch):
+def relay(dims, index_hbm, buffer_ref, gain_ref, gate_hbm, up_hbm, down_hbm, out_ref, *scratch):
     ns, nd, ticks, rows, width, gate_chunks, gate_cols, down_chunks, down_cols = dims
     nz = nd // 2
     scratch = list(scratch)
@@ -31,7 +31,8 @@
     downs = [scratch.pop(0) for _ in range(down_chunks)]
     (blocks, normed, hidden, partial, paired, summed, landed, advanced,
      gate_sem, up_sem, down_sem, spread_send, forward_send, block_recv,
-     pair_send, pair_recv, row_send, row_recv, shift_send, shift_recv) = scratch
+     pair_send, pair_recv, row_send, row_recv, shift_send, shift_recv,
+     residual, index_ref, index_sem, ready) = scratch
 
     s = lax.axis_index("section")
     d = lax.axis_index("dp")
@@ -47,6 +48,8 @@
     def at(zz):
         return zz * 2 + core
 
+    index_load = pltpu.make_async_copy(index_hbm, index_ref, index_sem)
+    index_load.start()
     loads = []
     for i in range(gate_chunks):
         cols = pl.ds(i * gate_cols, gate_cols)
@@ -62,11 +65,10 @@
     pl.semaphore_signal(barrier, inc=1, device_id=dev(s, other), device_id_type=MESH)
     for j in range(1, nz):
         pl.semaphore_signal(barrier, inc=1, device_id=dev(s, at(flipped(z, j))), device_id_type=MESH)
-    for j in range(nz):
-        zz = flipped(z, j)
-        pl.semaphore_signal(barrier, inc=1, device_id=dev(after, at(zz)), device_id_type=MESH)
-        pl.semaphore_signal(barrier, inc=1, device_id=dev(before, at(zz)), device_id_type=MESH)
-    pl.semaphore_wait(barrier, 3 * nz)
+    for section in (after, before):
+        pl.semaphore_signal(barrier, inc=1, device_id=dev(section, d), device_id_type=MESH)
+    pl.semaphore_wait(barrier, nz + 2)
+    pl.semaphore_signal(ready, inc=1, device_id=dev(before, d), device_id_type=MESH)
 
     sent = []
 
@@ -84,8 +86,11 @@
             device_id=dev(s, other), device_id_type=MESH,
         ).wait_recv()
 
+    def await_section():
+        pl.semaphore_wait(ready, 1)
+
     for t in range(ticks):
-        layer = index_ref[t, 0]
+        last = t == ticks - 1
         if t == 0:
             for j in reversed(range(1, nz)):
                 send(buffer_ref.at[0], blocks.at[t, d], spread_send.at[t, j], block_recv.at[t, d],
@@ -93,6 +98,8 @@
             send(buffer_ref.at[0], blocks.at[t, d], forward_send.at[t, 0], block_recv.at[t, d], dev(s, other))
             blocks[t, d] = buffer_ref[0]
         else:
+            if t == 1:
+                await_section()
             for j in reversed(range(nz)):
                 send(advanced.at[t - 1], blocks.at[t, d], spread_send.at[t, j], block_recv.at[t, d],
                      dev(after, at(flipped(z, j))))
@@ -102,6 +109,14 @@
                 arrived(blocks.at[t, slot], block_recv.at[t, slot])
                 send(blocks.at[t, slot], blocks.at[t, slot], forward_send.at[t, j], block_recv.at[t, slot],
                      dev(s, other))
+        if last:
+            if t == 0:
+                await_section()
+            kept = buffer_ref.at[0] if t == 0 else blocks.at[t, d]
+            send(kept, residual, shift_send, shift_recv, dev(after, d))
+        if t == 0:
+            index_load.wait()
+        layer = index_ref[t, 0]
         gain = gain_ref[0, pl.ds(layer, 1), :]
         for j in range(nz):
             zz = flipped(z, j)
@@ -127,10 +142,10 @@
         def scatter(c):
             arrived(paired.at[t, c], pair_recv.at[t, c])
             summed[t, c] = (partial[t, c, core] + paired[t, c]).astype(jnp.bfloat16)
-            for j in reversed(range(1, nz)):
+            for j in reversed(range(0 if last else 1, nz)):
                 zz = flipped(z, j)
                 send(summed.at[t, c, zz], landed.at[t, c, z], row_send.at[t, c, j], row_recv.at[t, c, z],
-                     dev(s, at(zz)))
+                     dev(after if last else s, at(zz)))
 
         for c in range(down_chunks):
             if t == 0:
@@ -145,17 +160,23 @@
                 scatter(c - 1)
         scatter(down_chunks - 1)
 
+        if last:
+            arrived(residual, shift_recv)
         for c in range(down_chunks):
-            total = partial[t, c, core, z] + paired[t, c, z]
-            for j in range(1, nz):
+            cols = slice(c * down_cols, (c + 1) * down_cols)
+            if last:
+                total = residual[:, cols].astype(jnp.float32)
+            else:
+                total = blocks[t, d, :, cols].astype(jnp.float32) + partial[t, c, core, z] + paired[t, c, z]
+            for j in range(0 if last else 1, nz):
                 zz = flipped(z, j)
                 arrived(landed.at[t, c, zz], row_recv.at[t, c, zz])
                 total = total + landed[t, c, zz].astype(jnp.float32)
-            cols = slice(c * down_cols, (c + 1) * down_cols)
-            advanced[t, :, cols] = (blocks[t, d, :, cols].astype(jnp.float32) + total).astype(jnp.bfloat16)
-
-    send(advanced.at[ticks - 1], out_ref.at[0], shift_send, shift_recv, dev(after, d))
-    arrived(out_ref.at[0], shift_recv)
+            if last:
+                out_ref[0, :, cols] = total.astype(jnp.bfloat16)
+            else:
+                advanced[t, :, cols] = total.astype(jnp.bfloat16)
+
     for copy in sent:
         copy.wait_send()
 
@@ -189,15 +210,16 @@
             DMA((ticks, down_chunks)), DMA((ticks, down_chunks)),
             DMA((ticks, down_chunks, nz)), DMA((ticks, down_chunks, nz)),
             DMA, DMA,
+            pltpu.VMEM((rows, width), bf16), pltpu.SMEM((ticks, 1), jnp.int32), DMA,
+            pltpu.SemaphoreType.REGULAR,
         ]
     )
     vmem = pl.BlockSpec(memory_space=pltpu.VMEM)
-    smem = pl.BlockSpec(memory_space=pltpu.SMEM)
     hbm = pl.BlockSpec(memory_space=pl.ANY)
     return pl.pallas_call(
         functools.partial(relay, dims),
         out_shape=jax.ShapeDtypeStruct(buffer.shape, buffer.dtype),
-        in_specs=[smem, vmem, vmem, hbm, hbm, hbm],
+        in_specs=[hbm, vmem, vmem, hbm, hbm, hbm],
         out_specs=vmem,
         scratch_shapes=scratch,
         compiler_params=pltpu.CompilerParams(

time: 42.9 us -> 38 us (0.89)
  Pallas kernels: 40 us -> 35.1 us
    pallas_call x1, Pallas kernels: 40 us -> 35.1 us  [on_device(): pl.pallas_call(functools.partial(relay, dims), out_shape=jax.ShapeDtypeSt...]
where the time goes in v2:
time: 38 us; the launch traced here: 37.8 us
  Pallas kernels  35.1 us (92%)
  local copies, waits for them, and re-layouts  2.67 us (7%)
    pallas_call x1, Pallas kernels, on_device(): pl.pallas_call(functools.partial(relay, dims), out_shape=jax.ShapeDtypeSt...  35.1 us
    unnamed x2, local copies, waits for them, and re-layouts  2.67 us

profile of v2, /device:TPU:0, one launch (start us, length us, event | category | flops | bytes accessed | tf_op | source)
XLA Modules:
  0.0 37.8 jit_solution(15813551052985740206)
XLA Ops:
  0.0 1.3 %copy.7.index_hbm = s32[2,1]{1,0:T(2,128)} copy(s32[2,1]{0,1:T(1,128)} %param.11) | data formatting | bytes 16 | tf_op args[5]
  1.3 35.1 %shard_map.64 = bf16[1,8,2048]{2,1,0:T(8,128)(2,1)} custom-call(s32[2,1]{1,0:T(2,128)} %copy.7.index_hbm, bf16[1,8,2048]{2,1,0:T(8,128)(2,1)} %buffer_ref.1, f32[1,2,2048]{2,1,0:T(2,128)} %gain_ref.1, bf16[1,2,2048,1024]{3,2,1,0:T(8,128)(2,1)} %gate_hbm.1, bf16[1,2,2048,1024]{3,2,1,0:T(8,128)(2,1)} %up_hbm.1, bf16[1,2,1024,2048]{3,2,1,0:T(8,128)(2,1)} %down_hbm.1), custom_call_target="tpu_custom_call" | custom-call | tf_op jit(solution)/shard_map/pallas_call | solution.py:219
  36.4 1.4 %copy.9 = bf16[1,8,2048]{2,1,0:T(8,128)(2,1)} copy(bf16[1,8,2048]{2,1,0:T(8,128)(2,1)} %shard_map.64) | data formatting | bytes 65536
